TPU v7x, 8 devices: a whole 2x2x1 slice. The times are simulated.
8 devices in a mesh: data: 2 (over z, y), tp: 4 (over x, core).
Axes of the slice: x: 2, y: 2, z: 1, core: 2. Of those that a mesh axis runs over, the one named last changes fastest.
Arguments:
- x_one: bfloat16 [1024, 49152], P('data', 'tp'), parts along dimension 0
- x_two: bfloat16 [1024, 49152], P('data', 'tp'), parts along dimension 0
- w_down: bfloat16 [49152, 12288], P('tp')
Outputs:
- output 1: bfloat16 [1024, 12288], P('data'), parts along dimension 0
- output 2: bfloat16 [1024, 12288], P('data'), parts along dimension 0
There are 2 independent parts. A program takes and returns all parts, laid end to end along the dimension named above; an argument that names none is the same for every part.
All inputs are finite; a program needn't handle non-finite values.
Results may differ from a plain program's by a relative error of at most 0.001.
Values are sent between devices in bfloat16 or wider.
A program may use at most 1.5 GiB of HBM per device.

v0:
```python
import jax
import jax.numpy as jnp
from jax import lax
from jax.sharding import PartitionSpec as P


def solution(mesh):
    def per_device(x_one, x_two, w_down):
        part_one = jnp.dot(x_one, w_down, preferred_element_type=jnp.float32)
        part_two = jnp.dot(x_two, w_down, preferred_element_type=jnp.float32)
        y_one = lax.psum(part_one, "tp").astype(jnp.bfloat16)
        y_two = lax.psum(part_two, "tp").astype(jnp.bfloat16)
        return y_one, y_two

    return jax.shard_map(
        per_device,
        mesh=mesh,
        in_specs=(P("data", "tp"), P("data", "tp"), P("tp", None)),
        out_specs=(P("data", None), P("data", None)),
        check_vma=False,
    )
```

profile of v0, /device:TPU:0, one launch (start us, length us, event | category | flops | bytes accessed | tf_op | source)
XLA Modules:
  0.0 1187.9 jit_solution(3120079281166098803)
XLA Ops:
  0.6 168.8 %fusion = f32[512,12288]{1,0:T(8,128)} fusion(bf16[512,12288]{1,0:T(8,128)(2,1)} %param.3, bf16[12288,12288]{1,0:T(8,128)(2,1)} %param.5), kind=kOutput, calls=%fused_computation | convolution fusion | flops 154618822656 | bytes 339738624 | tf_op jit(solution)/shard_map/dot_general | solution.py:9
  169.4 168.9 %fusion.1 = f32[512,12288]{1,0:T(8,128)} fusion(bf16[512,12288]{1,0:T(8,128)(2,1)} %param.4, bf16[12288,12288]{1,0:T(8,128)(2,1)} %param.5), kind=kOutput, calls=%fused_computation.1 | convolution fusion | flops 154618822656 | bytes 339738624 | tf_op jit(solution)/shard_map/dot_general | solution.py:10
  338.4 849.5 %all-reduce.2 = (bf16[512,12288]{1,0:T(8,128)(2,1)}, bf16[512,12288]{1,0:T(8,128)(2,1)}) all-reduce(f32[512,12288]{1,0:T(8,128)} %fusion, f32[512,12288]{1,0:T(8,128)} %fusion.1), channel_id=1, replica_groups=mesh['data'=2,'tp'=4] {'tp'}, use_global_device_ids=true, to_apply=%region_0.0 | all-reduce | flops 12582912 | bytes 75497472 | tf_op jit(solution)/shard_map/psum | solution.py:11
where the time goes:
time: 1190 us
  blocking collectives  849 us (71%)
  matrix products  338 us (28%)
    psum x1, blocking collectives, per_device(): y_one = lax.psum(part_one, 'tp').astype(jnp.bfloat16)  849 us
    dot_general x1, matrix products, per_device(): part_two = jnp.dot(x_two, w_down, preferred_element_type=jnp.float32)  169 us
    dot_general x1, matrix products, per_device(): part_one = jnp.dot(x_one, w_down, preferred_element_type=jnp.float32)  169 us

commit v1 on v0

v1 whole, which is shorter than its diff:
```python
import functools

import jax
import jax.numpy as jnp
from jax import lax
from jax.experimental import pallas as pl
from jax.experimental.pallas import tpu as pltpu
from jax.sharding import PartitionSpec as P

MESH = pl.DeviceIdType.MESH
LEAD = 3
BN = 256
KC = 6


def kernel(
    x_one, x_two, w, y_one, y_two,
    xbuf, wbuf, acc, pair, part, own, peer, total,
    x_sem, w_sem, pair_send, pair_recv, part_send, part_recv,
    y_local, y_pair_send, y_pair_recv, y_send, y_recv, fwd_send, fwd_recv,
):
    rows, width = x_one.shape
    cols = w.shape[1]
    kb = width // KC
    np_ = cols // BN // 2
    steps = 2 * np_
    big = 2 * steps
    n_part, n_peer, n_total = part.shape[0], peer.shape[0], total.shape[0]

    t = lax.axis_index("tp")
    chip, lane = lax.div(t, 2), lax.rem(t, 2)
    sibling = {"tp": 2 * chip + 1 - lane}
    across = {"tp": 2 * (1 - chip) + lane}

    def at_least(s, a):
        return lax.div(s + big - a, big)

    def is_peer(s):
        head = 1 - at_least(s, LEAD)
        tail = at_least(s, steps - LEAD)
        return head + (1 - head - tail) * lax.rem(s + LEAD + 2, 2)

    def index(s):
        head = 1 - at_least(s, LEAD)
        tail = at_least(s, steps - LEAD)
        mid = 1 - head - tail
        odd = lax.rem(s + LEAD + 2, 2)
        u = s - LEAD + big
        return head * s + tail * (s - np_) + mid * (lax.div(u, 2) - big // 2 + odd * LEAD)

    def columns(owner, j):
        return pl.ds(pl.multiple_of((owner * np_ + j) * BN, BN), BN)

    def block_columns(s):
        p = is_peer(s)
        return columns(chip + p * (1 - 2 * chip), index(s))

    def w_copy(s, k):
        return pltpu.make_async_copy(
            w.at[pl.ds(k * kb, kb), block_columns(s)], wbuf.at[k], w_sem.at[k]
        )

    def x_copy(k, m):
        x = (x_one, x_two)[m]
        return pltpu.make_async_copy(
            x.at[:, pl.ds(k * kb, kb)], xbuf.at[k, pl.ds(m * rows, rows)], x_sem.at[m, k]
        )

    def half(slot, which):
        return acc.at[slot, pl.ds(pl.multiple_of(which * rows, rows), rows)]

    def pair_copy(s):
        slot = lax.rem(s, 2)
        return pltpu.make_async_remote_copy(
            half(slot, 1 - lane), pair.at[slot], pair_send.at[slot], pair_recv.at[slot],
            device_id=sibling, device_id_type=MESH,
        )

    def part_copy(j):
        a, b = lax.rem(j, n_part), lax.rem(j, n_peer)
        return pltpu.make_async_remote_copy(
            part.at[a], peer.at[b], part_send.at[a], part_recv.at[b],
            device_id=across, device_id_type=MESH,
        )

    def y_copies(y, j):
        a = lax.rem(j, n_total)
        dst = y.at[:, columns(chip, j)]
        return (
            pltpu.make_async_remote_copy(
                total.at[a], dst, y_send.at[a], y_recv.at[j],
                device_id=across, device_id_type=MESH,
            ),
            pltpu.make_async_remote_copy(
                total.at[a], dst, y_pair_send.at[a], y_pair_recv.at[j],
                device_id=sibling, device_id_type=MESH,
            ),
            pltpu.make_async_copy(total.at[a], dst, y_local.at[a]),
        )

    def fwd_copy(y, j):
        ref = y.at[:, columns(1 - chip, j)]
        return pltpu.make_async_remote_copy(
            ref, ref, fwd_send.at[j], fwd_recv.at[j], device_id=sibling, device_id_type=MESH
        )

    def by_lane(f):
        @pl.when(lane == 0)
        def _():
            f(y_one)

        @pl.when(lane == 1)
        def _():
            f(y_two)

    def add_pair(s):
        slot = lax.rem(s, 2)
        p, j = is_peer(s), index(s)
        pair_copy(s).wait()

        @pl.when(p == 1)
        def _():
            @pl.when(j >= n_part)
            def _():
                part_copy(j - n_part).wait_send()

            part[lax.rem(j, n_part)] = half(slot, lane)[...] + pair[slot]

        @pl.when(p == 0)
        def _():
            own[lax.rem(j, 2)] = half(slot, lane)[...] + pair[slot]

    def send_part(s):
        @pl.when(is_peer(s) == 1)
        def _():
            part_copy(index(s)).start()

    def finish(j):
        part_copy(j).wait_recv()

        @pl.when(j >= n_total)
        def _():
            for c in y_copies(y_one, j - n_total)[:2]:
                c.wait_send()
            y_copies(y_one, j - n_total)[2].wait()

        total[lax.rem(j, n_total)] = (
            own[lax.rem(j, 2)] + peer[lax.rem(j, n_peer)]
        ).astype(jnp.bfloat16)

    def send_total(j):
        by_lane(lambda y: [c.start() for c in y_copies(y, j)] and None)

    def forward(j):
        y_copies(y_one, j)[0].wait_recv()
        by_lane(lambda y: fwd_copy(y, j).start())

    for k in range(KC):
        x_copy(k, 0).start()
        x_copy(k, 1).start()
        w_copy(0, k).start()

    barrier = pltpu.get_barrier_semaphore()
    for other in (sibling, across):
        pl.semaphore_signal(barrier, inc=1, device_id=other, device_id_type=MESH)
    pl.semaphore_wait(barrier, 2)

    def step(s, carry):
        slot = lax.rem(s, 2)
        before = jnp.maximum(s - 2, 0)

        def own_two_back(f):
            @pl.when(s >= 2)
            def _():
                @pl.when(is_peer(before) == 0)
                def _():
                    f(index(before))

        for k in range(KC):
            @pl.when(s == 0)
            def _():
                x_copy(k, 0).wait()
                x_copy(k, 1).wait()

            w_copy(s, k).wait()
            product = jnp.dot(xbuf[k], wbuf[k], preferred_element_type=jnp.float32)
            if k == 0:
                acc[slot] = product
            else:
                acc[slot] += product

            @pl.when(s + 1 < steps)
            def _():
                w_copy(s + 1, k).start()

            if k == 0:
                @pl.when(s >= 1)
                def _():
                    pair_copy(s - 1).start()
            if k == 2:
                @pl.when(s >= 1)
                def _():
                    add_pair(s - 1)
            if k == 3:
                @pl.when(s >= 1)
                def _():
                    send_part(s - 1)

                own_two_back(finish)
            if k == 4:
                own_two_back(send_total)
            if k == 5:
                @pl.when(s >= 2)
                def _():
                    @pl.when(is_peer(before) == 0)
                    def _():
                        @pl.when(index(before) >= LEAD + 1)
                        def _():
                            forward(index(before) - LEAD - 1)
        return carry

    lax.fori_loop(0, steps, step, 0)

    last = steps - 1
    pair_copy(last).start()
    finish(np_ - 2)
    send_total(np_ - 2)
    add_pair(last)
    finish(np_ - 1)
    send_total(np_ - 1)
    for j in range(np_ - 2 - LEAD - 1, np_):
        forward(j)

    for j in range(np_ - n_part, np_):
        part_copy(j).wait_send()
    for j in range(np_ - n_total, np_):
        for c in y_copies(y_one, j)[:2]:
            c.wait_send()
        y_copies(y_one, j)[2].wait()

    def drain(j, carry):
        y_copies(y_one, j)[1].wait_recv()
        fwd_copy(y_one, j).wait()
        return carry

    lax.fori_loop(0, np_, drain, 0)


def solution(mesh):
    def per_device(x_one, x_two, w_down):
        rows, width = x_one.shape
        cols = w_down.shape[1]
        blocks = cols // BN // 2
        n_part, n_peer, n_total = LEAD + 2, 2 * LEAD + 2, LEAD + 2
        dma = pltpu.SemaphoreType.DMA
        out = jax.ShapeDtypeStruct((rows, cols), jnp.bfloat16)
        any_ = pl.BlockSpec(memory_space=pl.ANY)
        return pl.pallas_call(
            kernel,
            out_shape=(out, out),
            in_specs=[any_] * 3,
            out_specs=(any_, any_),
            scratch_shapes=[
                pltpu.VMEM((KC, 2 * rows, width // KC), jnp.bfloat16),
                pltpu.VMEM((KC, width // KC, BN), jnp.bfloat16),
                pltpu.VMEM((2, 2 * rows, BN), jnp.float32),
                pltpu.VMEM((2, rows, BN), jnp.float32),
                pltpu.VMEM((n_part, rows, BN), jnp.float32),
                pltpu.VMEM((2, rows, BN), jnp.float32),
                pltpu.VMEM((n_peer, rows, BN), jnp.float32),
                pltpu.VMEM((n_total, rows, BN), jnp.bfloat16),
                dma((2, KC)),
                dma((KC,)),
                dma((2,)),
                dma((2,)),
                dma((n_part,)),
                dma((n_peer,)),
                dma((n_total,)),
                dma((n_total,)),
                dma((blocks,)),
                dma((n_total,)),
                dma((blocks,)),
                dma((blocks,)),
                dma((blocks,)),
            ],
            compiler_params=pltpu.CompilerParams(
                collective_id=0, has_side_effects=True, vmem_limit_bytes=58 * 1024 * 1024
            ),
            cost_estimate=pl.CostEstimate(
                flops=4 * rows * width * cols,
                bytes_accessed=2 * width * cols,
                transcendentals=0,
            ),
        )(x_one, x_two, w_down)

    return jax.shard_map(
        per_device,
        mesh=mesh,
        in_specs=(P("data", "tp"), P("data", "tp"), P("tp", None)),
        out_specs=(P("data", None), P("data", None)),
        check_vma=False,
    )
```

time: 1190 us -> 698 us (0.59)
  blocking collectives: 849 us -> 0 us
  Pallas kernels: 0 us -> 679 us
  matrix products: 338 us -> 0 us
  local copies, waits for them, and re-layouts: 0 us -> 17.7 us
    psum x1 -> x0, blocking collectives: 849 us -> none  [per_device(): y_one = lax.psum(part_one, 'tp').astype(jnp.bfloat16)]
    pallas_call x0 -> x1, Pallas kernels: none -> 679 us  [per_device(): pl.pallas_call(kernel, out_shape=(out, out), in_specs=[any_] * 3, out_spe...]
    dot_general x2 -> x0, matrix products: 338 us -> none  [the longest x1 169 us: per_device(): part_two = jnp.dot(x_two, w_down, preferred_element_type=jnp.float32)]
    unnamed x0 -> x4, local copies, waits for them, and re-layouts: none -> 17.7 us
where the time goes in v1:
time: 698 us
  Pallas kernels  679 us (97%)
  local copies, waits for them, and re-layouts  17.7 us (3%)
    pallas_call x1, Pallas kernels, per_device(): pl.pallas_call(kernel, out_shape=(out, out), in_specs=[any_] * 3, out_spe...  679 us
    unnamed x4, local copies, waits for them, and re-layouts  17.7 us

profile of v1, /device:TPU:0, one launch (start us, length us, event | category | flops | bytes accessed | tf_op | source)
XLA Modules:
  0.0 697.6 jit_solution(9957465063162146368)
XLA Ops:
  0.6 679.3 %shard_map.50 = (bf16[512,12288]{1,0:T(8,128)(2,1)}, bf16[512,12288]{1,0:T(8,128)(2,1)}) custom-call(bf16[512,12288]{1,0:T(8,128)(2,1)} %x_one.1, bf16[512,12288]{1,0:T(8,128)(2,1)} %x_two.1, bf16[12288,12288]{1,0:T(8,128)(2,1)} %w.1), custom_call_target="tpu_custom_call" | custom-call | flops 309237645312 | bytes 301989888 | tf_op jit(solution)/shard_map/pallas_call | solution.py:258
  679.9 0.0 copy-start
  679.9 11.3 %copy.7 = bf16[512,12288]{1,0:T(8,128)(2,1)} copy(bf16[512,12288]{1,0:T(8,128)(2,1)} %get-tuple-element.4) | data formatting | bytes 25165824
  691.2 1.6 copy-done
  692.8 4.8 copy.8
Async XLA Ops:
  679.9 12.9 %copy-start = (bf16[512,12288]{1,0:T(8,128)(2,1)S(1)}, bf16[512,12288]{1,0:T(8,128)(2,1)}, u32[]{:S(2)}) copy-start(bf16[512,12288]{1,0:T(8,128)(2,1)} %get-tuple-element.5) | copy-start | bytes 37748740

commit v2 on v1

--- a/solution.py
+++ b/solution.py
@@ -183,11 +183,12 @@
                 x_copy(k, 1).wait()
 
             w_copy(s, k).wait()
-            product = jnp.dot(xbuf[k], wbuf[k], preferred_element_type=jnp.float32)
-            if k == 0:
-                acc[slot] = product
-            else:
-                acc[slot] += product
+            for m in range(2):
+                product = jnp.dot(xbuf[k, m * rows : (m + 1) * rows], wbuf[k], preferred_element_type=jnp.float32)
+                if k == 0:
+                    acc[slot, m * rows : (m + 1) * rows] = product
+                else:
+                    acc[slot, m * rows : (m + 1) * rows] += product
 
             @pl.when(s + 1 < steps)
             def _():

time: 698 us -> 446 us (0.64)
  Pallas kernels: 679 us -> 428 us
    pallas_call x1, Pallas kernels: 679 us -> 428 us  [per_device(): pl.pallas_call(kernel, out_shape=(out, out), in_specs=[any_] * 3, out_spe...]
where the time goes in v2:
time: 446 us
  Pallas kernels  428 us (96%)
  local copies, waits for them, and re-layouts  17.7 us (4%)
    pallas_call x1, Pallas kernels, per_device(): pl.pallas_call(kernel, out_shape=(out, out), in_specs=[any_] * 3, out_spe...  428 us
    unnamed x4, local copies, waits for them, and re-layouts  17.7 us

profile of v2, /device:TPU:0, one launch (start us, length us, event | category | flops | bytes accessed | tf_op | source)
XLA Modules:
  0.0 446.2 jit_solution(8234240200160136680)
XLA Ops:
  0.6 427.9 %shard_map.50 = (bf16[512,12288]{1,0:T(8,128)(2,1)}, bf16[512,12288]{1,0:T(8,128)(2,1)}) custom-call(bf16[512,12288]{1,0:T(8,128)(2,1)} %x_one.1, bf16[512,12288]{1,0:T(8,128)(2,1)} %x_two.1, bf16[12288,12288]{1,0:T(8,128)(2,1)} %w.1), custom_call_target="tpu_custom_call" | custom-call | flops 309237645312 | bytes 301989888 | tf_op jit(solution)/shard_map/pallas_call | solution.py:259
  428.5 0.0 copy-start
  428.5 11.3 %copy.7 = bf16[512,12288]{1,0:T(8,128)(2,1)} copy(bf16[512,12288]{1,0:T(8,128)(2,1)} %get-tuple-element.4) | data formatting | bytes 25165824
  439.8 1.6 copy-done
  441.4 4.8 %copy.8 = bf16[512,12288]{1,0:T(8,128)(2,1)} copy(bf16[512,12288]{1,0:T(8,128)(2,1)S(1)} %copy-done) | data formatting | bytes 25165824
Async XLA Ops:
  428.5 12.9 %copy-start = (bf16[512,12288]{1,0:T(8,128)(2,1)S(1)}, bf16[512,12288]{1,0:T(8,128)(2,1)}, u32[]{:S(2)}) copy-start(bf16[512,12288]{1,0:T(8,128)(2,1)} %get-tuple-element.5) | copy-start | bytes 37748740

commit v3 on v2

v3 whole, which is shorter than its diff:
```python
import jax
import jax.numpy as jnp
from jax import lax
from jax.experimental import pallas as pl
from jax.experimental.pallas import tpu as pltpu
from jax.sharding import PartitionSpec as P

MESH = pl.DeviceIdType.MESH
LEAD = 3
BN = 256
KC = 6
LATE = 8


def kernel(
    x_one, x_two, w, y_one, y_two, h_one, h_two,
    wbuf, acc, pair, part, own, peer, total,
    x_sem, w_sem, pair_send, pair_recv, part_send, part_recv,
    y_local, y_pair_send, y_pair_recv, y_send, y_recv, fwd_send, fwd_recv,
    back_sem, late_sem, free_sem,
):
    rows, width = x_one.shape
    cols = w.shape[1]
    kb = width // KC
    np_ = cols // BN // 2
    steps = 2 * np_
    big = 2 * steps
    n_part, n_peer, n_total = part.shape[0], peer.shape[0], total.shape[0]
    early = np_ - LATE

    t = lax.axis_index("tp")
    chip, lane = lax.div(t, 2), lax.rem(t, 2)
    sibling = {"tp": 2 * chip + 1 - lane}
    across = {"tp": 2 * (1 - chip) + lane}

    def at_least(s, a):
        return lax.div(s + big - a, big)

    def is_peer(s):
        head = 1 - at_least(s, LEAD)
        tail = at_least(s, steps - LEAD)
        return head + (1 - head - tail) * lax.rem(s + LEAD + 2, 2)

    def index(s):
        head = 1 - at_least(s, LEAD)
        tail = at_least(s, steps - LEAD)
        mid = 1 - head - tail
        odd = lax.rem(s + LEAD + 2, 2)
        u = s - LEAD + big
        return head * s + tail * (s - np_) + mid * (lax.div(u, 2) - big // 2 + odd * LEAD)

    def columns(owner, j, n=1):
        return pl.ds(pl.multiple_of((owner * np_ + j) * BN, BN), n * BN)

    def block_columns(s):
        p = is_peer(s)
        return columns(chip + p * (1 - 2 * chip), index(s))

    def w_copy(s, k):
        return pltpu.make_async_copy(
            w.at[pl.ds(k * kb, kb), block_columns(s)], wbuf.at[k], w_sem.at[k]
        )

    def x_copy(k, m):
        x, y = ((x_one, y_one), (x_two, y_two))[m]
        at = pl.ds(k * kb, kb)
        return pltpu.make_async_copy(x.at[:, at], y.at[:, at], x_sem.at[m, k])

    def x_rows(k, m, lo, n):
        return (y_one, y_two)[m][lo : lo + n, k * kb : (k + 1) * kb]

    def half(slot, which):
        return acc.at[slot, pl.ds(pl.multiple_of(which * rows, rows), rows)]

    def pair_copy(s):
        slot = lax.rem(s, 2)
        return pltpu.make_async_remote_copy(
            half(slot, 1 - lane), pair.at[slot], pair_send.at[slot], pair_recv.at[slot],
            device_id=sibling, device_id_type=MESH,
        )

    def part_copy(j):
        a, b = lax.rem(j, n_part), lax.rem(j, n_peer)
        return pltpu.make_async_remote_copy(
            part.at[a], peer.at[b], part_send.at[a], part_recv.at[b],
            device_id=across, device_id_type=MESH,
        )

    def y_across(y, j):
        a = lax.rem(j, n_total)
        return pltpu.make_async_remote_copy(
            total.at[a], y.at[:, columns(chip, j)], y_send.at[a], y_recv.at[j],
            device_id=across, device_id_type=MESH,
        )

    def y_pair(y, j):
        a = lax.rem(j, n_total)
        return pltpu.make_async_remote_copy(
            total.at[a], y.at[:, columns(chip, j)], y_pair_send.at[a], y_pair_recv.at[j],
            device_id=sibling, device_id_type=MESH,
        )

    def y_here(y, j):
        a = lax.rem(j, n_total)
        return pltpu.make_async_copy(total.at[a], y.at[:, columns(chip, j)], y_local.at[a])

    def fwd_copy(y, j):
        ref = y.at[:, columns(1 - chip, j)]
        return pltpu.make_async_remote_copy(
            ref, ref, fwd_send.at[j], fwd_recv.at[j], device_id=sibling, device_id_type=MESH
        )

    def back_copy(h, y, owner, j, n, sem):
        at = columns(owner, j, n)
        return pltpu.make_async_copy(h.at[:, at], y.at[:, at], sem)

    def by_lane(f, which=None):
        which = lane if which is None else which

        @pl.when(which == 0)
        def _():
            f(h_one, y_one)

        @pl.when(which == 1)
        def _():
            f(h_two, y_two)

    def add_pair(s):
        slot = lax.rem(s, 2)
        p, j = is_peer(s), index(s)
        pair_copy(s).wait_recv()

        @pl.when(p == 1)
        def _():
            @pl.when(j >= n_part)
            def _():
                part_copy(j - n_part).wait_send()

            part[lax.rem(j, n_part)] = half(slot, lane)[...] + pair[slot]
            part_copy(j).start()

        @pl.when(p == 0)
        def _():
            own[lax.rem(j, 2)] = half(slot, lane)[...] + pair[slot]

    def wait_total(j):
        y_across(h_one, j).wait_send()
        y_pair(h_one, j).wait_send()
        y_here(h_one, j).wait()

    def finish(j):
        part_copy(j).wait_recv()

        @pl.when(j >= n_total)
        def _():
            wait_total(j - n_total)

        total[lax.rem(j, n_total)] = (
            own[lax.rem(j, 2)] + peer[lax.rem(j, n_peer)]
        ).astype(jnp.bfloat16)

    def send_total(j):
        def send(h, y):
            y_across(h, j).start()
            y_pair(h, j).start()
            y_here(h, j).start()

        by_lane(send)

    def forward(j):
        y_across(h_one, j).wait_recv()
        by_lane(lambda h, y: fwd_copy(h, j).start())

    for k in range(KC):
        x_copy(k, 0).start()
        w_copy(0, k).start()

    barrier = pltpu.get_barrier_semaphore()
    for other in (sibling, across):
        pl.semaphore_signal(barrier, inc=1, device_id=other, device_id_type=MESH)
    pl.semaphore_wait(barrier, 2)

    quarter = rows // 2
    for m in range(2):
        for k in range(KC):
            x_copy(k, m).wait()
            if m == 0:
                w_copy(0, k).wait()
                if k >= KC // 2:
                    x_copy(2 * k - KC, 1).start()
                    x_copy(2 * k - KC + 1, 1).start()
            for q in range(2):
                at = pl.ds(m * rows + q * quarter, quarter)
                product = jnp.dot(
                    x_rows(k, m, q * quarter, quarter), wbuf[k],
                    preferred_element_type=jnp.float32,
                )
                if k == 0:
                    acc[0, at] = product
                else:
                    acc[0, at] += product
            if m == 1:
                w_copy(1, k).start()
                if k == 2:
                    @pl.when(lane == 0)
                    def _():
                        add_pair(0)

        @pl.when(lane == 1 - m)
        def _():
            pair_copy(0).start()

    def step(s, carry):
        slot = lax.rem(s, 2)
        before = jnp.maximum(s - 2, 0)

        def own_two_back(f):
            @pl.when(s >= 2)
            def _():
                @pl.when(is_peer(before) == 0)
                def _():
                    f(index(before))

        def forward_behind(j):
            @pl.when(j >= LEAD + 1)
            def _():
                forward(j - LEAD - 1)

        for k in range(KC):
            w_copy(s, k).wait()
            for m in range(2):
                at = pl.ds(m * rows, rows)
                product = jnp.dot(
                    x_rows(k, m, 0, rows), wbuf[k], preferred_element_type=jnp.float32
                )
                if k == 0:
                    acc[slot, at] = product
                else:
                    acc[slot, at] += product

            @pl.when(s + 1 < steps)
            def _():
                w_copy(s + 1, k).start()

            if k == 1:
                pair_copy(s - 1).wait_send()

                @pl.when(s + lane >= 2)
                def _():
                    add_pair(s - 1)
            if k == 2:
                own_two_back(finish)
            if k == 3:
                own_two_back(send_total)
            if k == 4:
                own_two_back(forward_behind)

        pair_copy(s).start()
        return carry

    lax.fori_loop(1, steps, step, 0)

    for other in (sibling, across):
        pl.semaphore_signal(free_sem, inc=1, device_id=other, device_id_type=MESH)

    def landed(j, carry):
        y_pair(h_one, j).wait_recv()
        fwd_copy(h_one, j).wait_recv()
        return carry

    lax.fori_loop(0, early, landed, 0)
    bulk = [
        back_copy(h, y, owner, 0, early, back_sem.at[m, owner])
        for m, (h, y) in enumerate(((h_one, y_one), (h_two, y_two)))
        for owner in range(2)
    ]
    for c in bulk:
        c.start()

    last = np_ - 1
    pair_copy(steps - 1).wait_send()
    add_pair(steps - 1)
    for j in range(np_ - 2 - LEAD - 1, last - LEAD):
        forward(j)
    finish(last - 1)
    send_total(last - 1)
    forward(last - LEAD - 1 + 1)
    finish(last)
    pl.semaphore_wait(free_sem, 2)

    def send_last(h, y):
        y_across(y, last).start()
        y_pair(y, last).start()
        y[:, columns(chip, last)] = total[last % n_total]

    by_lane(send_last)

    for j in range(np_ - n_total, last):
        y_here(h_one, j).wait()
    by_lane(lambda h, y: back_copy(h, y, chip, early, LATE - 1, late_sem.at[0]).start())
    for j in range(early, np_):
        y_pair(h_one, j).wait_recv()
    by_lane(
        lambda h, y: back_copy(h, y, chip, early, LATE - 1, late_sem.at[1]).start(), 1 - lane
    )

    for j in range(last - LEAD + 1, last):
        forward(j)
    by_lane(lambda h, y: back_copy(h, y, 1 - chip, early, LATE - 1, late_sem.at[2]).start())
    for j in range(early, last):
        fwd_copy(h_one, j).wait_recv()
    by_lane(
        lambda h, y: back_copy(h, y, 1 - chip, early, LATE - 1, late_sem.at[3]).start(), 1 - lane
    )
    y_across(y_one, last).wait_recv()
    by_lane(lambda h, y: fwd_copy(y, last).start())

    for c in bulk:
        c.wait()
    for a in range(4):
        back_copy(h_one, y_one, 0, early, LATE - 1, late_sem.at[a]).wait()
    for j in range(np_ - n_part, np_):
        part_copy(j).wait_send()
    for j in range(np_ - n_total, np_):
        y_across(h_one, j).wait_send()
        y_pair(h_one, j).wait_send()

    def sent(j, carry):
        fwd_copy(h_one, j).wait_send()
        return carry

    lax.fori_loop(0, np_, sent, 0)
    fwd_copy(y_one, last).wait_recv()


def solution(mesh):
    def per_device(x_one, x_two, w_down):
        rows, width = x_one.shape
        cols = w_down.shape[1]
        blocks = cols // BN // 2
        n_part, n_peer, n_total = LEAD + 2, 2 * LEAD + 2, LEAD + 2
        dma = pltpu.SemaphoreType.DMA
        out = jax.ShapeDtypeStruct((rows, cols), jnp.bfloat16)
        hbm = pl.BlockSpec(memory_space=pltpu.HBM)
        vmem = pl.BlockSpec(memory_space=pltpu.VMEM)
        return pl.pallas_call(
            kernel,
            out_shape=(out, out, out, out),
            in_specs=[hbm] * 3,
            out_specs=(vmem, vmem, hbm, hbm),
            scratch_shapes=[
                pltpu.VMEM((KC, width // KC, BN), jnp.bfloat16),
                pltpu.VMEM((2, 2 * rows, BN), jnp.float32),
                pltpu.VMEM((2, rows, BN), jnp.float32),
                pltpu.VMEM((n_part, rows, BN), jnp.float32),
                pltpu.VMEM((2, rows, BN), jnp.float32),
                pltpu.VMEM((n_peer, rows, BN), jnp.float32),
                pltpu.VMEM((n_total, rows, BN), jnp.bfloat16),
                dma((2, KC)),
                dma((KC,)),
                dma((2,)),
                dma((2,)),
                dma((n_part,)),
                dma((n_peer,)),
                dma((n_total,)),
                dma((n_total,)),
                dma((blocks,)),
                dma((n_total,)),
                dma((blocks,)),
                dma((blocks,)),
                dma((blocks,)),
                dma((2, 2)),
                dma((4,)),
                pltpu.SemaphoreType.REGULAR,
            ],
            compiler_params=pltpu.CompilerParams(
                collective_id=0, has_side_effects=True, vmem_limit_bytes=24 * 1024 * 1024
            ),
            cost_estimate=pl.CostEstimate(
                flops=4 * rows * width * cols,
                bytes_accessed=2 * width * cols,
                transcendentals=0,
            ),
        )(x_one, x_two, w_down)[:2]

    return jax.shard_map(
        per_device,
        mesh=mesh,
        in_specs=(P("data", "tp"), P("data", "tp"), P("tp", None)),
        out_specs=(P("data", None), P("data", None)),
        check_vma=False,
    )
```

time: 446 us -> 432 us (0.969)
  local copies, waits for them, and re-layouts: 17.7 us -> 9.56 us
  Pallas kernels: 428 us -> 421 us
    unnamed x4 -> x2, local copies, waits for them, and re-layouts: 17.7 us -> 9.56 us
    pallas_call x1, Pallas kernels: 428 us -> 421 us  [per_device(): pl.pallas_call(kernel, out_shape=(out, out, out, out), in_specs=[hbm] * 3...]
where the time goes in v3:
time: 432 us; the launch traced here: 431 us
  Pallas kernels  421 us (97%)
  local copies, waits for them, and re-layouts  9.56 us (2%)
    pallas_call x1, Pallas kernels, per_device(): pl.pallas_call(kernel, out_shape=(out, out, out, out), in_specs=[hbm] * 3...  421 us
    unnamed x2, local copies, waits for them, and re-layouts  9.56 us

profile of v3, /device:TPU:0, one launch (start us, length us, event | category | flops | bytes accessed | tf_op | source)
XLA Modules:
  0.0 431.5 jit_solution(1023957702177989874)
XLA Ops:
  0.6 421.3 %shard_map.50 = (bf16[512,12288]{1,0:T(8,128)(2,1)S(1)}, bf16[512,12288]{1,0:T(8,128)(2,1)S(1)}, bf16[512,12288]{1,0:T(8,128)(2,1)}, bf16[512,12288]{1,0:T(8,128)(2,1)}) custom-call(bf16[512,12288]{1,0:T(8,128)(2,1)} %x_one.1, bf16[512,12288]{1,0:T(8,128)(2,1)} %x_two.1, bf16[12288,12288]{1,0:T(8,128)(2,1)} %w.1), custom_call_target="tpu_custom_call" | custom-call | flops 309237645312 | bytes 301989888 | tf_op jit(solution)/shard_map/pallas_call | solution.py:346
  421.9 4.8 %copy.7 = bf16[512,12288]{1,0:T(8,128)(2,1)} copy(bf16[512,12288]{1,0:T(8,128)(2,1)S(1)} %get-tuple-element.8) | data formatting | bytes 25165824
  426.7 4.8 %copy.8 = bf16[512,12288]{1,0:T(8,128)(2,1)} copy(bf16[512,12288]{1,0:T(8,128)(2,1)S(1)} %get-tuple-element.9) | data formatting | bytes 25165824

commit v4 on v3

--- a/solution.py
+++ b/solution.py
@@ -6,9 +6,11 @@
 from jax.sharding import PartitionSpec as P
 
 MESH = pl.DeviceIdType.MESH
-LEAD = 3
+LEAD = 4
 BN = 256
 KC = 6
+AHEAD = 4
+PIECES = 8
 LATE = 8
 
 
@@ -17,7 +19,7 @@
     wbuf, acc, pair, part, own, peer, total,
     x_sem, w_sem, pair_send, pair_recv, part_send, part_recv,
     y_local, y_pair_send, y_pair_recv, y_send, y_recv, fwd_send, fwd_recv,
-    back_sem, late_sem, free_sem,
+    back_sem, late_sem, first_send, first_recv, free_sem,
 ):
     rows, width = x_one.shape
     cols = w.shape[1]
@@ -27,6 +29,7 @@
     big = 2 * steps
     n_part, n_peer, n_total = part.shape[0], peer.shape[0], total.shape[0]
     early = np_ - LATE
+    quarter = rows // 2
 
     t = lax.axis_index("tp")
     chip, lane = lax.div(t, 2), lax.rem(t, 2)
@@ -61,10 +64,10 @@
             w.at[pl.ds(k * kb, kb), block_columns(s)], wbuf.at[k], w_sem.at[k]
         )
 
-    def x_copy(k, m):
+    def x_copy(k, m, q):
         x, y = ((x_one, y_one), (x_two, y_two))[m]
-        at = pl.ds(k * kb, kb)
-        return pltpu.make_async_copy(x.at[:, at], y.at[:, at], x_sem.at[m, k])
+        at = pl.ds(q * quarter, quarter), pl.ds(k * kb, kb)
+        return pltpu.make_async_copy(x.at[at], y.at[at], x_sem.at[m, q, k])
 
     def x_rows(k, m, lo, n):
         return (y_one, y_two)[m][lo : lo + n, k * kb : (k + 1) * kb]
@@ -171,55 +174,77 @@
         y_across(h_one, j).wait_recv()
         by_lane(lambda h, y: fwd_copy(h, j).start())
 
-    for k in range(KC):
-        x_copy(k, 0).start()
-        w_copy(0, k).start()
+    pieces = [(0, m, q * quarter, quarter) for m in range(2) for q in range(2)]
+    pieces += [(1, m, 0, rows) for m in range(2)]
+
+    def piece_copy(s, m, lo, n):
+        q = lo // quarter
+        send, recv = (first_send.at[q], first_recv.at[q]) if s == 0 else (
+            pair_send.at[1], pair_recv.at[1])
+        return pltpu.make_async_remote_copy(
+            acc.at[s, pl.ds(m * rows + lo, n)], pair.at[s, pl.ds(lo, n)], send, recv,
+            device_id=sibling, device_id_type=MESH,
+        )
+
+    def add_piece(s, m, lo, n):
+        @pl.when(lane == m)
+        def _():
+            at = pl.ds(lo, n)
+            piece_copy(s, m, lo, n).wait_recv()
+            part[s, at] = acc[s, pl.ds(m * rows + lo, n)] + pair[s, at]
+            pltpu.make_async_remote_copy(
+                part.at[s, at], peer.at[s, at], part_send.at[s], part_recv.at[s],
+                device_id=across, device_id_type=MESH,
+            ).start()
+
+    loads = [(x_copy(k, 0, 0), w_copy(0, k)) for k in range(KC)]
+    loads += [(x_copy(k, m, q),) for m, q in ((0, 1), (1, 0), (1, 1)) for k in range(KC)]
+    loads += [(w_copy(1, k),) for k in range(KC)]
+    for load in loads[:AHEAD]:
+        for c in load:
+            c.start()
 
     barrier = pltpu.get_barrier_semaphore()
     for other in (sibling, across):
         pl.semaphore_signal(barrier, inc=1, device_id=other, device_id_type=MESH)
     pl.semaphore_wait(barrier, 2)
 
-    quarter = rows // 2
-    for m in range(2):
+    for i, (s, m, lo, n) in enumerate(pieces):
         for k in range(KC):
-            x_copy(k, m).wait()
-            if m == 0:
-                w_copy(0, k).wait()
-                if k >= KC // 2:
-                    x_copy(2 * k - KC, 1).start()
-                    x_copy(2 * k - KC + 1, 1).start()
-            for q in range(2):
-                at = pl.ds(m * rows + q * quarter, quarter)
+            now = i * KC + k
+            for c in loads[now] if now < len(loads) else ():
+                c.wait()
+            for c in loads[now + AHEAD] if now + AHEAD < len(loads) else ():
+                c.start()
+            for d in range(2):
+                at = pl.ds(m * rows + lo + d * n // 2, n // 2)
                 product = jnp.dot(
-                    x_rows(k, m, q * quarter, quarter), wbuf[k],
+                    x_rows(k, m, lo + d * n // 2, n // 2), wbuf[k],
                     preferred_element_type=jnp.float32,
                 )
                 if k == 0:
-                    acc[0, at] = product
+                    acc[s, at] = product
                 else:
-                    acc[0, at] += product
-            if m == 1:
-                w_copy(1, k).start()
-                if k == 2:
-                    @pl.when(lane == 0)
-                    def _():
-                        add_pair(0)
+                    acc[s, at] += product
+            if i == len(pieces) - 1:
+                w_copy(2, k).start()
+            if i > 0 and k == (4 if n == quarter else 2):
+                add_piece(*pieces[i - 1])
 
         @pl.when(lane == 1 - m)
         def _():
-            pair_copy(0).start()
+            piece_copy(s, m, lo, n).start()
+
+    for q in range(2):
+        piece_copy(0, 0, q * quarter, quarter).wait_send()
 
     def step(s, carry):
         slot = lax.rem(s, 2)
-        before = jnp.maximum(s - 2, 0)
 
         def own_two_back(f):
-            @pl.when(s >= 2)
+            @pl.when(is_peer(s - 2) == 0)
             def _():
-                @pl.when(is_peer(before) == 0)
-                def _():
-                    f(index(before))
+                f(index(s - 2))
 
         def forward_behind(j):
             @pl.when(j >= LEAD + 1)
@@ -245,7 +270,7 @@
             if k == 1:
                 pair_copy(s - 1).wait_send()
 
-                @pl.when(s + lane >= 2)
+                @pl.when(s + lane >= 3)
                 def _():
                     add_pair(s - 1)
             if k == 2:
@@ -258,7 +283,7 @@
         pair_copy(s).start()
         return carry
 
-    lax.fori_loop(1, steps, step, 0)
+    lax.fori_loop(2, steps, step, 0)
 
     for other in (sibling, across):
         pl.semaphore_signal(free_sem, inc=1, device_id=other, device_id_type=MESH)
@@ -333,6 +358,21 @@
     fwd_copy(y_one, last).wait_recv()
 
 
+def to_result(a, b, y_one, y_two, sem):
+    rows = a.shape[0] // PIECES
+    copies = [
+        pltpu.make_async_copy(
+            src.at[pl.ds(i * rows, rows)], dst.at[pl.ds(i * rows, rows)], sem.at[m, i]
+        )
+        for i in range(PIECES)
+        for m, (src, dst) in enumerate(((a, y_one), (b, y_two)))
+    ]
+    for c in copies:
+        c.start()
+    for c in copies:
+        c.wait()
+
+
 def solution(mesh):
     def per_device(x_one, x_two, w_down):
         rows, width = x_one.shape
@@ -343,7 +383,7 @@
         out = jax.ShapeDtypeStruct((rows, cols), jnp.bfloat16)
         hbm = pl.BlockSpec(memory_space=pltpu.HBM)
         vmem = pl.BlockSpec(memory_space=pltpu.VMEM)
-        return pl.pallas_call(
+        y_one, y_two = pl.pallas_call(
             kernel,
             out_shape=(out, out, out, out),
             in_specs=[hbm] * 3,
@@ -356,7 +396,7 @@
                 pltpu.VMEM((2, rows, BN), jnp.float32),
                 pltpu.VMEM((n_peer, rows, BN), jnp.float32),
                 pltpu.VMEM((n_total, rows, BN), jnp.bfloat16),
-                dma((2, KC)),
+                dma((2, 2, KC)),
                 dma((KC,)),
                 dma((2,)),
                 dma((2,)),
@@ -371,6 +411,8 @@
                 dma((blocks,)),
                 dma((2, 2)),
                 dma((4,)),
+                dma((2,)),
+                dma((2,)),
                 pltpu.SemaphoreType.REGULAR,
             ],
             compiler_params=pltpu.CompilerParams(
@@ -382,6 +424,17 @@
                 transcendentals=0,
             ),
         )(x_one, x_two, w_down)[:2]
+        return pl.pallas_call(
+            to_result,
+            out_shape=(out, out),
+            in_specs=[vmem] * 2,
+            out_specs=(hbm, hbm),
+            scratch_shapes=[dma((2, PIECES))],
+            compiler_params=pltpu.CompilerParams(vmem_limit_bytes=1024 * 1024),
+            cost_estimate=pl.CostEstimate(
+                flops=0, bytes_accessed=8 * rows * cols, transcendentals=0
+            ),
+        )(y_one, y_two)
 
     return jax.shard_map(
         per_device,

time: 432 us -> 428 us (level)
  local copies, waits for them, and re-layouts: 9.56 us -> 0 us
  Pallas kernels: 421 us -> 427 us
    unnamed x2 -> x0, local copies, waits for them, and re-layouts: 9.56 us -> none
    pallas_call x0 -> x1, Pallas kernels: none -> 8.51 us  [per_device(): pl.pallas_call(to_result, out_shape=(out, out), in_specs=[vmem] * 2, out_...]
where the time goes in v4:
time: 428 us
  Pallas kernels  427 us (100%)
    pallas_call x1, Pallas kernels, per_device(): pl.pallas_call(kernel, out_shape=(out, out, out, out), in_specs=[hbm] * 3...  419 us

profile of v4, /device:TPU:0, one launch (start us, length us, event | category | flops | bytes accessed | tf_op | source)
XLA Modules:
  0.0 428.2 jit_solution(16893201872826992895)
XLA Ops:
  0.6 418.9 %shard_map.50 = (bf16[512,12288]{1,0:T(8,128)(2,1)S(1)}, bf16[512,12288]{1,0:T(8,128)(2,1)S(1)}, bf16[512,12288]{1,0:T(8,128)(2,1)}, bf16[512,12288]{1,0:T(8,128)(2,1)}) custom-call(bf16[512,12288]{1,0:T(8,128)(2,1)} %x_one.1, bf16[512,12288]{1,0:T(8,128)(2,1)} %x_two.1, bf16[12288,12288]{1,0:T(8,128)(2,1)} %w.1), custom_call_target="tpu_custom_call" | custom-call | flops 309237645312 | bytes 301989888 | tf_op jit(solution)/shard_map/pallas_call | solution.py:386
  419.6 8.5 %shard_map.51 = (bf16[512,12288]{1,0:T(8,128)(2,1)}, bf16[512,12288]{1,0:T(8,128)(2,1)}) custom-call(bf16[512,12288]{1,0:T(8,128)(2,1)S(1)} %get-tuple-element.4.a, bf16[512,12288]{1,0:T(8,128)(2,1)S(1)} %get-tuple-element.5.b), custom_call_target="tpu_custom_call" | custom-call | bytes 50331648 | tf_op jit(solution)/shard_map/pallas_call | solution.py:427

commit v5 on v4

--- a/solution.py
+++ b/solution.py
@@ -11,6 +11,7 @@
 KC = 6
 AHEAD = 4
 PIECES = 8
+LAST = 4
 LATE = 8
 
 
@@ -19,7 +20,7 @@
     wbuf, acc, pair, part, own, peer, total,
     x_sem, w_sem, pair_send, pair_recv, part_send, part_recv,
     y_local, y_pair_send, y_pair_recv, y_send, y_recv, fwd_send, fwd_recv,
-    back_sem, late_sem, first_send, first_recv, free_sem,
+    back_sem, late_sem, first_send, first_recv, last_recv, free_sem,
 ):
     rows, width = x_one.shape
     cols = w.shape[1]
@@ -207,7 +208,6 @@
     barrier = pltpu.get_barrier_semaphore()
     for other in (sibling, across):
         pl.semaphore_signal(barrier, inc=1, device_id=other, device_id_type=MESH)
-    pl.semaphore_wait(barrier, 2)
 
     for i, (s, m, lo, n) in enumerate(pieces):
         for k in range(KC):
@@ -231,6 +231,9 @@
             if i > 0 and k == (4 if n == quarter else 2):
                 add_piece(*pieces[i - 1])
 
+        if i == 0:
+            pl.semaphore_wait(barrier, 2)
+
         @pl.when(lane == 1 - m)
         def _():
             piece_copy(s, m, lo, n).start()
@@ -313,8 +316,26 @@
     finish(last)
     pl.semaphore_wait(free_sem, 2)
 
+    cut = rows // LAST
+
+    def last_across(y, i):
+        at = pl.ds(i * cut, cut)
+        return pltpu.make_async_remote_copy(
+            total.at[last % n_total, at], y.at[at, columns(chip, last)],
+            y_send.at[last % n_total], last_recv.at[i],
+            device_id=across, device_id_type=MESH,
+        )
+
+    def last_fwd(y, i):
+        ref = y.at[pl.ds(i * cut, cut), columns(1 - chip, last)]
+        return pltpu.make_async_remote_copy(
+            ref, ref, fwd_send.at[last], fwd_recv.at[last],
+            device_id=sibling, device_id_type=MESH,
+        )
+
     def send_last(h, y):
-        y_across(y, last).start()
+        for i in range(LAST):
+            last_across(y, i).start()
         y_pair(y, last).start()
         y[:, columns(chip, last)] = total[last % n_total]
 
@@ -337,8 +358,9 @@
     by_lane(
         lambda h, y: back_copy(h, y, 1 - chip, early, LATE - 1, late_sem.at[3]).start(), 1 - lane
     )
-    y_across(y_one, last).wait_recv()
-    by_lane(lambda h, y: fwd_copy(y, last).start())
+    for i in range(LAST):
+        last_across(y_one, i).wait_recv()
+        by_lane(lambda h, y: last_fwd(y, i).start())
 
     for c in bulk:
         c.wait()
@@ -413,6 +435,7 @@
                 dma((4,)),
                 dma((2,)),
                 dma((2,)),
+                dma((LAST,)),
                 pltpu.SemaphoreType.REGULAR,
             ],
             compiler_params=pltpu.CompilerParams(

time: 428 us -> 428 us (level)
  no operation moved by 1% of the time
where the time goes in v5:
time: 428 us
  Pallas kernels  427 us (100%)
    pallas_call x1, Pallas kernels, per_device(): pl.pallas_call(kernel, out_shape=(out, out, out, out), in_specs=[hbm] * 3...  419 us

profile of v5, /device:TPU:0, one launch (start us, length us, event | category | flops | bytes accessed | tf_op | source)
XLA Modules:
  0.0 428.0 jit_solution(7254490960419182020)
XLA Ops:
  0.6 418.7 %shard_map.50 = (bf16[512,12288]{1,0:T(8,128)(2,1)S(1)}, bf16[512,12288]{1,0:T(8,128)(2,1)S(1)}, bf16[512,12288]{1,0:T(8,128)(2,1)}, bf16[512,12288]{1,0:T(8,128)(2,1)}) custom-call(bf16[512,12288]{1,0:T(8,128)(2,1)} %x_one.1, bf16[512,12288]{1,0:T(8,128)(2,1)} %x_two.1, bf16[12288,12288]{1,0:T(8,128)(2,1)} %w.1), custom_call_target="tpu_custom_call" | custom-call | flops 309237645312 | bytes 301989888 | tf_op jit(solution)/shard_map/pallas_call | solution.py:408
  419.3 8.5 %shard_map.51 = (bf16[512,12288]{1,0:T(8,128)(2,1)}, bf16[512,12288]{1,0:T(8,128)(2,1)}) custom-call(bf16[512,12288]{1,0:T(8,128)(2,1)S(1)} %get-tuple-element.4.a, bf16[512,12288]{1,0:T(8,128)(2,1)S(1)} %get-tuple-element.5.b), custom_call_target="tpu_custom_call" | custom-call | bytes 50331648 | tf_op jit(solution)/shard_map/pallas_call | solution.py:450

commit v6 on v5

--- a/solution.py
+++ b/solution.py
@@ -9,8 +9,8 @@
 LEAD = 4
 BN = 256
 KC = 6
-AHEAD = 4
-PIECES = 8
+AHEAD = 5
+PIECES = 4
 LAST = 4
 LATE = 8
 
@@ -228,7 +228,7 @@
                     acc[s, at] += product
             if i == len(pieces) - 1:
                 w_copy(2, k).start()
-            if i > 0 and k == (4 if n == quarter else 2):
+            if i > 0 and k == (3 if n == quarter else 2):
                 add_piece(*pieces[i - 1])
 
         if i == 0:

time: 428 us -> 428 us (level)
  no operation moved by 1% of the time
where the time goes in v6:
time: 428 us
  Pallas kernels  427 us (100%)
    pallas_call x1, Pallas kernels, per_device(): pl.pallas_call(kernel, out_shape=(out, out, out, out), in_specs=[hbm] * 3...  418 us

profile of v6, /device:TPU:0, one launch (start us, length us, event | category | flops | bytes accessed | tf_op | source)
XLA Modules:
  0.0 427.6 jit_solution(17968128674482646273)
XLA Ops:
  0.6 418.3 %shard_map.50 = (bf16[512,12288]{1,0:T(8,128)(2,1)S(1)}, bf16[512,12288]{1,0:T(8,128)(2,1)S(1)}, bf16[512,12288]{1,0:T(8,128)(2,1)}, bf16[512,12288]{1,0:T(8,128)(2,1)}) custom-call(bf16[512,12288]{1,0:T(8,128)(2,1)} %x_one.1, bf16[512,12288]{1,0:T(8,128)(2,1)} %x_two.1, bf16[12288,12288]{1,0:T(8,128)(2,1)} %w.1), custom_call_target="tpu_custom_call" | custom-call | flops 309237645312 | bytes 301989888 | tf_op jit(solution)/shard_map/pallas_call | solution.py:408
  418.9 8.5 %shard_map.51 = (bf16[512,12288]{1,0:T(8,128)(2,1)}, bf16[512,12288]{1,0:T(8,128)(2,1)}) custom-call(bf16[512,12288]{1,0:T(8,128)(2,1)S(1)} %get-tuple-element.4.a, bf16[512,12288]{1,0:T(8,128)(2,1)S(1)} %get-tuple-element.5.b), custom_call_target="tpu_custom_call" | custom-call | bytes 50331648 | tf_op jit(solution)/shard_map/pallas_call | solution.py:450
